TPU v7x, 128 devices: a whole 4x4x4 slice. The times are simulated.
128 devices in a mesh: pb: 8 (over z, core), ka: 16 (over x, y).
Axes of the slice: x: 4, y: 4, z: 4, core: 2. Of those that a mesh axis runs over, the one named last changes fastest.
Arguments:
- queries: float32 [1, 16384, 128], P(None, ('pb', 'ka')), may hold values from -6 to 6
- keys: float32 [1, 16384, 128], P(None, ('ka', 'pb')), may hold values from -6 to 6
- values: float32 [1, 16384, 128], P(None, ('ka', 'pb')), may hold values from -6 to 6
- tangent_q: float32 [1, 16384, 128], P(None, ('pb', 'ka')), may hold values from -6 to 6
- tangent_k: float32 [1, 16384, 128], P(None, ('ka', 'pb')), may hold values from -6 to 6
- tangent_v: float32 [1, 16384, 128], P(None, ('ka', 'pb')), may hold values from -6 to 6
Outputs:
- attended: float32 [1, 16384, 128], P(None, ('pb', 'ka'))
- attended_tangent: float32 [1, 16384, 128], P(None, ('pb', 'ka'))
All inputs are finite; a program needn't handle non-finite values.
Results may differ from a plain program's by a relative error of at most 0.0003.
Values sent between devices are 32-bit elements; how exact they have to be, the bound alone decides.
A program may use at most 128 MiB of HBM per device.

v0:
```python
import functools
import math

import jax
import jax.numpy as jnp
from jax import lax
from jax.sharding import Mesh
from jax.sharding import PartitionSpec as P

KA = ("ka_0", "ka_1")
PB_KA = ("pb", "ka_0", "ka_1")
KA_PB = ("ka_0", "ka_1", "pb")


def sent_together(arrays, axis, dim, along):
    ends, at = ([], 0)
    for a in arrays[:-1]:
        at += a.shape[along]
        ends.append(at)
    both = jnp.concatenate(arrays, axis=along)
    return tuple(jnp.split(lax.all_gather(both, axis, axis=dim, tiled=True), ends, axis=along))


def by_axis(x, axes):
    return functools.reduce(lax.pmax, axes, x)


def split_up(x, dim, peers):
    before, after = (x.shape[:dim], x.shape[dim + 1 :])
    return jnp.moveaxis(x.reshape(*before, peers, -1, *after), dim, 0)


def sum_at_owner(x, axis, dim):
    peers = lax.axis_size(axis)
    blocks = lax.all_to_all(split_up(x, dim, peers), axis, 0, 0, tiled=True)
    return jnp.sum(blocks, axis=0)


def sent_together_2(arrays, axis, dim, along):
    widths = [math.prod(a.shape[along:]) for a in arrays]
    both = jnp.concatenate(
        [a.reshape(*a.shape[:along], w) for a, w in zip(arrays, widths)], axis=along
    )
    out = sum_at_owner(both, axis, dim)
    blocks = jnp.split(out, [sum(widths[:k]) for k in range(1, len(widths))], axis=along)
    return tuple((b.reshape(*out.shape[:along], *a.shape[along:]) for a, b in zip(arrays, blocks)))


def body(queries, keys, values, tangent_q, tangent_k, tangent_v):
    highest = lax.Precision.HIGHEST
    head_count, _, width = queries.shape
    factor = width ** (-0.5)
    all_q, all_dq = sent_together((queries, tangent_q), KA, 1, 0)
    span = all_q.shape[1]
    block = min(512, span)
    blocks = span // block
    split_q = all_q.reshape(head_count, blocks, block, width)
    split_dq = all_dq.reshape(head_count, blocks, block, width)
    start_state = (
        jnp.full((head_count, span), -1e30, jnp.float32),
        jnp.zeros((head_count, span), jnp.float32),
        jnp.zeros((head_count, span, width), jnp.float32),
        jnp.zeros((head_count, span, width), jnp.float32),
        jnp.zeros((head_count, span), jnp.float32),
    )
    piece_k, piece_dk, piece_v, piece_dv = sent_together(
        (keys, tangent_k, values, tangent_v), "pb", 1, 0
    )
    shaped = (
        start_state[0].reshape(head_count, blocks, block),
        start_state[1].reshape(head_count, blocks, block),
        start_state[2].reshape(head_count, blocks, block, width),
        start_state[3].reshape(head_count, blocks, block, width),
        start_state[4].reshape(head_count, blocks, block),
    )

    def one_head(items):
        (
            head_q,
            head_dq,
            head_k,
            head_dk,
            head_v,
            head_dv,
            peak_h,
            total_h,
            numer_h,
            tnumer_h,
            drift_h,
        ) = items

        def one_block(parts):
            query_blk, dquery_blk, old_peak, old_total, old_numer, old_tnumer, old_drift = parts
            scores = jnp.dot(query_blk, head_k.T, precision=highest) * factor
            tangent = (
                jnp.dot(dquery_blk, head_k.T, precision=highest)
                + jnp.dot(query_blk, head_dk.T, precision=highest)
            ) * factor
            new_peak = jnp.maximum(old_peak, jnp.max(scores, axis=1))
            rescale = jnp.exp(old_peak - new_peak)
            weights = jnp.exp(scores - new_peak[:, None])
            product = weights * tangent
            new_total = old_total * rescale + jnp.sum(weights, axis=1)
            new_numer = old_numer * rescale[:, None] + jnp.dot(weights, head_v, precision=highest)
            new_tnumer = (
                old_tnumer * rescale[:, None]
                + jnp.dot(weights, head_dv, precision=highest)
                + jnp.dot(product, head_v, precision=highest)
            )
            new_drift = old_drift * rescale + jnp.sum(product, axis=1)
            return (new_peak, new_total, new_numer, new_tnumer, new_drift)

        return lax.map(one_block, (head_q, head_dq, peak_h, total_h, numer_h, tnumer_h, drift_h))

    result = lax.map(one_head, (split_q, split_dq, piece_k, piece_dk, piece_v, piece_dv) + shaped)
    peak = result[0].reshape(head_count, span)
    total = result[1].reshape(head_count, span)
    numer = result[2].reshape(head_count, span, width)
    tnumer = result[3].reshape(head_count, span, width)
    drift = result[4].reshape(head_count, span)
    global_peak = by_axis(peak, KA)
    rescale = jnp.exp(peak - global_peak)
    total, numer, tnumer, drift = sent_together_2(
        (total * rescale, numer * rescale[..., None], tnumer * rescale[..., None], drift * rescale),
        KA,
        1,
        2,
    )
    attended = numer / total[..., None]
    attended_tangent = tnumer / total[..., None] - attended * (drift / total)[..., None]
    return (attended, attended_tangent)


def solution(mesh):
    finer = Mesh(mesh.devices.reshape(mesh.shape["pb"], 4, 4), ("pb", "ka_0", "ka_1"))
    placed = (
        P(None, PB_KA, None),
        P(None, KA_PB, None),
        P(None, KA_PB, None),
        P(None, PB_KA, None),
        P(None, KA_PB, None),
        P(None, KA_PB, None),
    )
    return jax.shard_map(
        body,
        mesh=finer,
        in_specs=placed,
        out_specs=(P(None, PB_KA, None), P(None, PB_KA, None)),
        check_vma=False,
    )
```

profile of v0, /device:TPU:0, one launch (start us, length us, event | category | flops | bytes accessed | tf_op | source)
XLA Modules:
  0.0 226.6 jit_solution(10836296284399147957)
XLA Ops:
  7.2 1.6 pad_maximum_fusion.1
  8.9 1.5 pad_maximum_fusion.2
  10.5 27.2 %all-gather.5.cloned.1.call-done = f32[4,1024,128]{2,1,0:T(8,128)} async-done(((f32[4,128,128]{2,1,0:T(8,128)}), f32[4,1024,128]{2,1,0:T(8,128)}) %all-gather.5.cloned.1.call-update) | async-done | bytes 2097168 | tf_op jit(solution)/shard_map/all_gather | solution.py:21
  37.7 2.7 %slice_bitcast_fusion = (f32[1024,128]{1,0:T(8,128)}, f32[1024,128]{1,0:T(8,128)}, f32[1024,128]{1,0:T(8,128)S(1)}, f32[1024,128]{1,0:T(8,128)S(1)}) fusion(f32[4,1024,128]{2,1,0:T(8,128)} %all-gather.5.cloned.1.call-done), kind=kLoop, calls=%fused_computation.28 | loop fusion | bytes 4194304 | tf_op jit(solution)/shard_map/while/body/jit(dynamic_index_in_dim)/squeeze | solution.py:115
  40.4 44.5 %all-gather.3.cloned.1.call-done = f32[2,2048,128]{2,1,0:T(8,128)} async-done(((f32[2,128,128]{2,1,0:T(8,128)}), f32[2,2048,128]{2,1,0:T(8,128)}) %all-gather.3.cloned.1.call-update) | async-done | bytes 2097168 | tf_op jit(solution)/shard_map/all_gather | solution.py:21
  84.9 3.0 %fusion.22 = (f32[1,2048,128]{2,1,0:T(8,128)}, f32[1,2048,128]{2,1,0:T(8,128)}) fusion(f32[2,2048,128]{2,1,0:T(8,128)} %all-gather.3.cloned.1.call-done), kind=kLoop, calls=%fused_computation.45 | loop fusion | bytes 4194304 | tf_op jit(solution)/shard_map/split | solution.py:21
  87.8 73.3 %while.35 = (s32[]{:T(128)}, f32[4,512]{1,0:T(4,128)S(1)}, f32[4,512]{1,0:T(4,128)S(1)}, f32[4,512,128]{2,1,0:T(8,128)}, f32[4,512,128]{2,1,0:T(8,128)}, /*index...) while((s32[]{:T(128)}, f32[4,512]{1,0:T(4,128)S(1)}, ...), condition=%wide.region_4.5_spmd, body=%wide.region_0.4_spmd.sunk | while | flops 4839901184 | bytes 36485376 | solution.py:113
  87.8 2.9 %multiply_reduce_fusion.2 = (f32[512]{0:T(512)S(1)}, f32[512,1024]{1,0:T(8,128)S(1)}) fusion(f32[1024,128]{1,0:T(8,128)S(1)} %get-tuple-element.388, f32[4,512,128]{2,1,0:T(8,128)} %get-tuple-element.387, s32[]{:T(128)S(6)} %copy.35), kind=kOutput, calls=%fused_computation.2.clone.1 | convolution fusion | flops 806354432 | bytes 2885636 | tf_op jit(solution)/shard_map/while/body/eval_jaxpr/while/body/eval_jaxpr/dot_general | solution.py:94
  90.8 2.8 %fusion.52 = f32[512,1024]{1,0:T(8,128)S(1)} fusion(f32[1024,128]{1,0:T(8,128)S(1)} %get-tuple-element.388, f32[4,512,128]{2,1,0:T(8,128)} %get-tuple-element.391, s32[]{:T(128)S(6)} %copy.35), kind=kOutput, calls=%fused_computation.10.clone.1 | convolution fusion | flops 805306368 | bytes 2883588 | tf_op jit(solution)/shard_map/while/body/eval_jaxpr/while/body/eval_jaxpr/dot_general | solution.py:96
  93.6 4.6 %fusion.53 = (f32[512]{0:T(512)S(1)}, f32[512,1024]{1,0:T(8,128)}) fusion(f32[512,1024]{1,0:T(8,128)S(1)} %fusion.52, f32[1024,128]{1,0:T(8,128)S(1)} %copy-done.1, f32[4,512,128]{2,1,0:T(8,128)} %get-tuple-element.387, s32[]{:T(128)S(6)} %copy.35, f32[512]{0:T(512)S(1)} %get-tuple-element.346, f32[512,1024]{1,0:T(8,128)S(1)} %get-tuple-element.347), kind=kOutput, calls=%fused_computation.44.clone.1 | convolution fusion | flops 808451584 | bytes 7081988 | tf_op jit(solution)/shard_map/while/body/eval_jaxpr/while/body/eval_jaxpr/dot_general | solution.py:97
  98.2 0.5 fusion.54
  98.8 2.7 %fusion.56 = f32[4,512,128]{2,1,0:T(8,128)} fusion(f32[4,512,128]{2,1,0:T(8,128)} %get-tuple-element.370, s32[]{:T(128)S(6)} %copy.35, f32[1024,128]{1,0:T(8,128)S(1)} %get-tuple-element.389, f32[512]{0:T(512)S(1)} %get-tuple-element.350, f32[512,1024]{1,0:T(8,128)S(1)} %get-tuple-element.347, f32[512]{0:T(512)S(1)} %get-tuple-element.346), kind=kOutput, calls=%fused_computation.9.clone.1 | convolution fusion | flops 806420480 | bytes 2887684 | tf_op jit(solution)/shard_map/while/body/eval_jaxpr/while/body/eval_jaxpr/dot_general | solution.py:104
  101.5 2.0 convolution_add_fusion.4
  103.5 2.5 %fusion.57 = f32[4,512,128]{2,1,0:T(8,128)} fusion(f32[4,512,128]{2,1,0:T(8,128)} %get-tuple-element.371, s32[]{:T(128)S(6)} %copy.35, f32[512,128]{1,0:T(8,128)S(1)} %convolution_add_fusion.4, f32[512,1024]{1,0:T(8,128)S(1)} %copy-done, f32[1024,128]{1,0:T(8,128)S(1)} %get-tuple-element.389), kind=kOutput, calls=%fused_computation.5.clone.1 | convolution fusion | flops 805371904 | bytes 3145732 | tf_op jit(solution)/shard_map/while/body/eval_jaxpr/while/body/eval_jaxpr/dot_general | solution.py:108
  106.1 2.9 %multiply_reduce_fusion.2 = (f32[512]{0:T(512)S(1)}, f32[512,1024]{1,0:T(8,128)S(1)}) fusion(f32[1024,128]{1,0:T(8,128)S(1)} %get-tuple-element.388, f32[4,512,128]{2,1,0:T(8,128)} %get-tuple-element.387, s32[]{:T(128)S(6)} %copy.35), kind=kOutput, calls=%fused_computation.2.clone.1 | convolution fusion | flops 806354432 | bytes 2885636 | tf_op jit(solution)/shard_map/while/body/eval_jaxpr/while/body/eval_jaxpr/dot_general | solution.py:94
  109.1 2.8 %fusion.52 = f32[512,1024]{1,0:T(8,128)S(1)} fusion(f32[1024,128]{1,0:T(8,128)S(1)} %get-tuple-element.388, f32[4,512,128]{2,1,0:T(8,128)} %get-tuple-element.391, s32[]{:T(128)S(6)} %copy.35), kind=kOutput, calls=%fused_computation.10.clone.1 | convolution fusion | flops 805306368 | bytes 2883588 | tf_op jit(solution)/shard_map/while/body/eval_jaxpr/while/body/eval_jaxpr/dot_general | solution.py:96
  111.9 4.6 %fusion.53 = (f32[512]{0:T(512)S(1)}, f32[512,1024]{1,0:T(8,128)}) fusion(f32[512,1024]{1,0:T(8,128)S(1)} %fusion.52, f32[1024,128]{1,0:T(8,128)S(1)} %copy-done.1, f32[4,512,128]{2,1,0:T(8,128)} %get-tuple-element.387, s32[]{:T(128)S(6)} %copy.35, f32[512]{0:T(512)S(1)} %get-tuple-element.346, f32[512,1024]{1,0:T(8,128)S(1)} %get-tuple-element.347), kind=kOutput, calls=%fused_computation.44.clone.1 | convolution fusion | flops 808451584 | bytes 7081988 | tf_op jit(solution)/shard_map/while/body/eval_jaxpr/while/body/eval_jaxpr/dot_general | solution.py:97
  116.5 0.5 fusion.54
  117.1 2.7 %fusion.56 = f32[4,512,128]{2,1,0:T(8,128)} fusion(f32[4,512,128]{2,1,0:T(8,128)} %get-tuple-element.370, s32[]{:T(128)S(6)} %copy.35, f32[1024,128]{1,0:T(8,128)S(1)} %get-tuple-element.389, f32[512]{0:T(512)S(1)} %get-tuple-element.350, f32[512,1024]{1,0:T(8,128)S(1)} %get-tuple-element.347, f32[512]{0:T(512)S(1)} %get-tuple-element.346), kind=kOutput, calls=%fused_computation.9.clone.1 | convolution fusion | flops 806420480 | bytes 2887684 | tf_op jit(solution)/shard_map/while/body/eval_jaxpr/while/body/eval_jaxpr/dot_general | solution.py:104
  119.8 2.0 convolution_add_fusion.4
  121.8 2.5 %fusion.57 = f32[4,512,128]{2,1,0:T(8,128)} fusion(f32[4,512,128]{2,1,0:T(8,128)} %get-tuple-element.371, s32[]{:T(128)S(6)} %copy.35, f32[512,128]{1,0:T(8,128)S(1)} %convolution_add_fusion.4, f32[512,1024]{1,0:T(8,128)S(1)} %copy-done, f32[1024,128]{1,0:T(8,128)S(1)} %get-tuple-element.389), kind=kOutput, calls=%fused_computation.5.clone.1 | convolution fusion | flops 805371904 | bytes 3145732 | tf_op jit(solution)/shard_map/while/body/eval_jaxpr/while/body/eval_jaxpr/dot_general | solution.py:108
  124.4 2.9 %multiply_reduce_fusion.2 = (f32[512]{0:T(512)S(1)}, f32[512,1024]{1,0:T(8,128)S(1)}) fusion(f32[1024,128]{1,0:T(8,128)S(1)} %get-tuple-element.388, f32[4,512,128]{2,1,0:T(8,128)} %get-tuple-element.387, s32[]{:T(128)S(6)} %copy.35), kind=kOutput, calls=%fused_computation.2.clone.1 | convolution fusion | flops 806354432 | bytes 2885636 | tf_op jit(solution)/shard_map/while/body/eval_jaxpr/while/body/eval_jaxpr/dot_general | solution.py:94
  127.4 2.8 %fusion.52 = f32[512,1024]{1,0:T(8,128)S(1)} fusion(f32[1024,128]{1,0:T(8,128)S(1)} %get-tuple-element.388, f32[4,512,128]{2,1,0:T(8,128)} %get-tuple-element.391, s32[]{:T(128)S(6)} %copy.35), kind=kOutput, calls=%fused_computation.10.clone.1 | convolution fusion | flops 805306368 | bytes 2883588 | tf_op jit(solution)/shard_map/while/body/eval_jaxpr/while/body/eval_jaxpr/dot_general | solution.py:96
  130.2 4.6 %fusion.53 = (f32[512]{0:T(512)S(1)}, f32[512,1024]{1,0:T(8,128)}) fusion(f32[512,1024]{1,0:T(8,128)S(1)} %fusion.52, f32[1024,128]{1,0:T(8,128)S(1)} %copy-done.1, f32[4,512,128]{2,1,0:T(8,128)} %get-tuple-element.387, s32[]{:T(128)S(6)} %copy.35, f32[512]{0:T(512)S(1)} %get-tuple-element.346, f32[512,1024]{1,0:T(8,128)S(1)} %get-tuple-element.347), kind=kOutput, calls=%fused_computation.44.clone.1 | convolution fusion | flops 808451584 | bytes 7081988 | tf_op jit(solution)/shard_map/while/body/eval_jaxpr/while/body/eval_jaxpr/dot_general | solution.py:97
  134.8 0.5 fusion.54
  135.4 2.7 %fusion.56 = f32[4,512,128]{2,1,0:T(8,128)} fusion(f32[4,512,128]{2,1,0:T(8,128)} %get-tuple-element.370, s32[]{:T(128)S(6)} %copy.35, f32[1024,128]{1,0:T(8,128)S(1)} %get-tuple-element.389, f32[512]{0:T(512)S(1)} %get-tuple-element.350, f32[512,1024]{1,0:T(8,128)S(1)} %get-tuple-element.347, f32[512]{0:T(512)S(1)} %get-tuple-element.346), kind=kOutput, calls=%fused_computation.9.clone.1 | convolution fusion | flops 806420480 | bytes 2887684 | tf_op jit(solution)/shard_map/while/body/eval_jaxpr/while/body/eval_jaxpr/dot_general | solution.py:104
  138.1 2.0 convolution_add_fusion.4
  140.1 2.5 %fusion.57 = f32[4,512,128]{2,1,0:T(8,128)} fusion(f32[4,512,128]{2,1,0:T(8,128)} %get-tuple-element.371, s32[]{:T(128)S(6)} %copy.35, f32[512,128]{1,0:T(8,128)S(1)} %convolution_add_fusion.4, f32[512,1024]{1,0:T(8,128)S(1)} %copy-done, f32[1024,128]{1,0:T(8,128)S(1)} %get-tuple-element.389), kind=kOutput, calls=%fused_computation.5.clone.1 | convolution fusion | flops 805371904 | bytes 3145732 | tf_op jit(solution)/shard_map/while/body/eval_jaxpr/while/body/eval_jaxpr/dot_general | solution.py:108
  142.7 2.9 %multiply_reduce_fusion.2 = (f32[512]{0:T(512)S(1)}, f32[512,1024]{1,0:T(8,128)S(1)}) fusion(f32[1024,128]{1,0:T(8,128)S(1)} %get-tuple-element.388, f32[4,512,128]{2,1,0:T(8,128)} %get-tuple-element.387, s32[]{:T(128)S(6)} %copy.35), kind=kOutput, calls=%fused_computation.2.clone.1 | convolution fusion | flops 806354432 | bytes 2885636 | tf_op jit(solution)/shard_map/while/body/eval_jaxpr/while/body/eval_jaxpr/dot_general | solution.py:94
  145.6 2.8 %fusion.52 = f32[512,1024]{1,0:T(8,128)S(1)} fusion(f32[1024,128]{1,0:T(8,128)S(1)} %get-tuple-element.388, f32[4,512,128]{2,1,0:T(8,128)} %get-tuple-element.391, s32[]{:T(128)S(6)} %copy.35), kind=kOutput, calls=%fused_computation.10.clone.1 | convolution fusion | flops 805306368 | bytes 2883588 | tf_op jit(solution)/shard_map/while/body/eval_jaxpr/while/body/eval_jaxpr/dot_general | solution.py:96
  148.5 4.6 %fusion.53 = (f32[512]{0:T(512)S(1)}, f32[512,1024]{1,0:T(8,128)}) fusion(f32[512,1024]{1,0:T(8,128)S(1)} %fusion.52, f32[1024,128]{1,0:T(8,128)S(1)} %copy-done.1, f32[4,512,128]{2,1,0:T(8,128)} %get-tuple-element.387, s32[]{:T(128)S(6)} %copy.35, f32[512]{0:T(512)S(1)} %get-tuple-element.346, f32[512,1024]{1,0:T(8,128)S(1)} %get-tuple-element.347), kind=kOutput, calls=%fused_computation.44.clone.1 | convolution fusion | flops 808451584 | bytes 7081988 | tf_op jit(solution)/shard_map/while/body/eval_jaxpr/while/body/eval_jaxpr/dot_general | solution.py:97
  153.1 0.5 fusion.54
  153.7 2.7 %fusion.56 = f32[4,512,128]{2,1,0:T(8,128)} fusion(f32[4,512,128]{2,1,0:T(8,128)} %get-tuple-element.370, s32[]{:T(128)S(6)} %copy.35, f32[1024,128]{1,0:T(8,128)S(1)} %get-tuple-element.389, f32[512]{0:T(512)S(1)} %get-tuple-element.350, f32[512,1024]{1,0:T(8,128)S(1)} %get-tuple-element.347, f32[512]{0:T(512)S(1)} %get-tuple-element.346), kind=kOutput, calls=%fused_computation.9.clone.1 | convolution fusion | flops 806420480 | bytes 2887684 | tf_op jit(solution)/shard_map/while/body/eval_jaxpr/while/body/eval_jaxpr/dot_general | solution.py:104
  156.4 2.0 convolution_add_fusion.4
  158.4 2.5 %fusion.57 = f32[4,512,128]{2,1,0:T(8,128)} fusion(f32[4,512,128]{2,1,0:T(8,128)} %get-tuple-element.371, s32[]{:T(128)S(6)} %copy.35, f32[512,128]{1,0:T(8,128)S(1)} %convolution_add_fusion.4, f32[512,1024]{1,0:T(8,128)S(1)} %copy-done, f32[1024,128]{1,0:T(8,128)S(1)} %get-tuple-element.389), kind=kOutput, calls=%fused_computation.5.clone.1 | convolution fusion | flops 805371904 | bytes 3145732 | tf_op jit(solution)/shard_map/while/body/eval_jaxpr/while/body/eval_jaxpr/dot_general | solution.py:108
  161.2 10.4 %pmax.14 = f32[1,2048]{1,0:T(1,128)S(1)} all-reduce(f32[1,2048]{1,0:T(1,128)S(1)} %bitcast.100), channel_id=1, replica_groups=mesh['pb'=8,'ka_0'=4,'ka_1'=4] {'ka_0'}, use_global_device_ids=true, to_apply=%region_5.6 | all-reduce | flops 2048 | bytes 16384 | tf_op jit(solution)/shard_map/pmax | solution.py:25
  171.6 8.7 %pmax.15 = f32[1,2048]{1,0:T(1,128)S(1)} all-reduce(f32[1,2048]{1,0:T(1,128)S(1)} %pmax.14), channel_id=1, replica_groups=mesh['pb'=8,'ka_0'=4,'ka_1'=4] {'ka_1'}, use_global_device_ids=true, to_apply=%region_6.7 | all-reduce | flops 2048 | bytes 16384 | tf_op jit(solution)/shard_map/pmax | solution.py:25
  180.3 1.3 copy.17
  181.7 1.4 copy.16
  183.1 0.4 broadcast_multiply_fusion.1
  183.5 0.8 copy-done.3
  184.3 0.3 copy-done.4
  184.6 1.4 pad_maximum_fusion
  186.0 3.8 %copy.18 = f32[16,1,128,258]{2,1,3,0:T(1,128)} copy(f32[16,1,128,258]{3,2,0,1:T(8,128)S(1)} %pad_maximum_fusion) | data formatting | bytes 4227072 | tf_op jit(solution)/shard_map/concatenate | solution.py:41
  189.9 27.1 %all_to_all.5 = f32[16,1,128,258]{2,1,3,0:T(1,128)S(1)} all-to-all(f32[16,1,128,258]{2,1,3,0:T(1,128)} %copy.18), channel_id=1, replica_groups=mesh['pb'=8,'ka_0'=4,'ka_1'=4] {'ka_0','ka_1'}, dimensions={0} | all-to-all | bytes 4227072 | tf_op jit(solution)/shard_map/all_to_all | solution.py:35
  216.9 1.3 reduce_sum.39
  218.3 0.7 copy.19
  219.0 0.7 copy.20
  (66 shorter events, 0.9 us)
Async XLA Ops:
  7.2 30.5 %all-gather.5.cloned.1.call-start = ((), (), s32[]{:S(2)}) async-start(), calls=%async_computation.2 | async-start | bytes 2359296 | tf_op jit(solution)/shard_map/all_gather | solution.py:21
  8.9 76.0 %all-gather.3.cloned.1.call-start = ((), (), s32[]{:S(2)}) async-start(), calls=%async_computation.1 | async-start | bytes 2228224 | tf_op jit(solution)/shard_map/all_gather | solution.py:21
  90.8 2.8 %copy-start.1 = (f32[1024,128]{1,0:T(8,128)S(1)}, f32[1024,128]{1,0:T(8,128)}, u32[]{:S(2)}) copy-start(f32[1024,128]{1,0:T(8,128)} %get-tuple-element.392) | copy-start | bytes 1572868 | tf_op jit(solution)/shard_map/while/body/eval_jaxpr/while
  98.8 2.7 %copy-start.2 = (f32[1024,128]{1,0:T(8,128)S(1)}, f32[1024,128]{1,0:T(8,128)}, u32[]{:S(2)}) copy-start(f32[1024,128]{1,0:T(8,128)} %get-tuple-element.390) | copy-start | bytes 1572868 | tf_op jit(solution)/shard_map/while/body/eval_jaxpr/while
  101.5 2.0 copy-start
  109.1 2.8 %copy-start.1 = (f32[1024,128]{1,0:T(8,128)S(1)}, f32[1024,128]{1,0:T(8,128)}, u32[]{:S(2)}) copy-start(f32[1024,128]{1,0:T(8,128)} %get-tuple-element.392) | copy-start | bytes 1572868 | tf_op jit(solution)/shard_map/while/body/eval_jaxpr/while
  117.1 2.7 %copy-start.2 = (f32[1024,128]{1,0:T(8,128)S(1)}, f32[1024,128]{1,0:T(8,128)}, u32[]{:S(2)}) copy-start(f32[1024,128]{1,0:T(8,128)} %get-tuple-element.390) | copy-start | bytes 1572868 | tf_op jit(solution)/shard_map/while/body/eval_jaxpr/while
  119.8 2.0 copy-start
  127.4 2.8 %copy-start.1 = (f32[1024,128]{1,0:T(8,128)S(1)}, f32[1024,128]{1,0:T(8,128)}, u32[]{:S(2)}) copy-start(f32[1024,128]{1,0:T(8,128)} %get-tuple-element.392) | copy-start | bytes 1572868 | tf_op jit(solution)/shard_map/while/body/eval_jaxpr/while
  135.4 2.7 %copy-start.2 = (f32[1024,128]{1,0:T(8,128)S(1)}, f32[1024,128]{1,0:T(8,128)}, u32[]{:S(2)}) copy-start(f32[1024,128]{1,0:T(8,128)} %get-tuple-element.390) | copy-start | bytes 1572868 | tf_op jit(solution)/shard_map/while/body/eval_jaxpr/while
  138.1 2.0 copy-start
  145.6 2.8 %copy-start.1 = (f32[1024,128]{1,0:T(8,128)S(1)}, f32[1024,128]{1,0:T(8,128)}, u32[]{:S(2)}) copy-start(f32[1024,128]{1,0:T(8,128)} %get-tuple-element.392) | copy-start | bytes 1572868 | tf_op jit(solution)/shard_map/while/body/eval_jaxpr/while
  153.6 2.7 %copy-start.2 = (f32[1024,128]{1,0:T(8,128)S(1)}, f32[1024,128]{1,0:T(8,128)}, u32[]{:S(2)}) copy-start(f32[1024,128]{1,0:T(8,128)} %get-tuple-element.390) | copy-start | bytes 1572868 | tf_op jit(solution)/shard_map/while/body/eval_jaxpr/while
  156.4 2.0 copy-start
  161.1 22.0 %copy-start.5 = (f32[4,512,128]{2,1,0:T(8,128)S(1)}, f32[4,512,128]{2,1,0:T(8,128)}, u32[]{:S(2)}) copy-start(f32[4,512,128]{2,1,0:T(8,128)} %get-tuple-element.213) | copy-start | bytes 3145732
  161.1 21.9 %copy-start.6 = (f32[4,512,128]{2,1,0:T(8,128)S(1)}, f32[4,512,128]{2,1,0:T(8,128)}, u32[]{:S(2)}) copy-start(f32[4,512,128]{2,1,0:T(8,128)} %get-tuple-element.214) | copy-start | bytes 3145732
  183.1 1.2 copy-start.3
  183.1 1.5 copy-start.4
Sparse Core Ops, SparseCore 0:
  9.7 28.0 all-gather.4
  39.9 44.9 all-gather.2
where the time goes:
time: 227 us
  waiting for transfers between devices  71.7 us (32%)
  matrix products  70.1 us (31%)
  blocking collectives  46.1 us (20%)
  local copies, waits for them, and re-layouts  15.5 us (7%)
  between operations  14.2 us (6%)
  other arithmetic  8.42 us (4%)
    all_gather x2, waiting for transfers between devices, sent_together(): lax.all_gather(both, axis, axis=dim, tiled=True)  71.7 us
    all_to_all x1, blocking collectives, sum_at_owner(): blocks = lax.all_to_all(split_up(x, dim, peers), axis, 0, 0, tiled=True)  27.1 us
    pmax x2, blocking collectives, by_axis(): return functools.reduce(lax.pmax, axes, x)  19 us
    dot_general x4, matrix products, one_block(): jnp.dot(query_blk, head_dk.T, precision=highest)  18.4 us
    dot_general x4, matrix products, one_block(): scores = jnp.dot(query_blk, head_k.T, precision=highest) * factor  11.6 us
    dot_general x4, matrix products, one_block(): jnp.dot(dquery_blk, head_k.T, precision=highest)  11.2 us
    dot_general x4, matrix products, one_block(): jnp.dot(weights, head_v, precision=highest)  10.9 us
    dot_general x4, matrix products, one_block(): jnp.dot(product, head_v, precision=highest)  10.1 us
  transfers between devices with their start and end apart: 2, of which 2 were waited for; matrix products, arithmetic and copies ran while one was open for 2% of the time, Pallas kernels for 0%

commit v1 on v0

v1 whole, which is shorter than its diff:
```python
import math

import jax
import jax.numpy as jnp
from jax import lax
from jax.experimental import pallas as pl
from jax.experimental.pallas import tpu as pltpu
from jax.sharding import PartitionSpec as P

F32, BF16 = jnp.float32, jnp.bfloat16
MESH = pl.DeviceIdType.MESH
B = 128
H = 64
ROWS, STATS = 136, 64
HALVES = ((0, 72), (72, 64))
LOG2E = math.log2(math.e)
LOTS = 47


def split(x):
    high = x.astype(BF16)
    return high, (x - high.astype(F32)).astype(BF16)


def dot(a, b):
    return jnp.dot(a, b, preferred_element_type=F32)


def kernel(
    q_ref, k_ref, v_ref, dq_ref, dk_ref, dv_ref, num_out, tan_out,
    q_in, k_in, qt, kb, vt, num, tan, num_in, tan_in, own_sem, send_sem, recv_sem,
):
    pb, ka = lax.axis_index("pb"), lax.axis_index("ka")
    z, core = pb // 2, pb % 2
    x, y = ka // 4, ka % 4
    x_up = {"ka": ((x + 1) % 4) * 4 + y, "pb": pb}
    x_down = {"ka": ((x + 3) % 4) * 4 + y, "pb": pb}
    z_up = {"ka": ka, "pb": ((z + 1) % 4) * 2 + core}
    z_down = {"ka": ka, "pb": ((z + 3) % 4) * 2 + core}
    q_pair = {"ka": x * 4 + y + 1 - 2 * (y % 2), "pb": pb}
    k_pair = {"ka": x * 4 + 3 - y, "pb": pb}
    twin = {"ka": ka, "pb": z * 2 + 1 - core}

    for src, dst in (
        (q_ref, q_in.at[0, 0]), (dq_ref, q_in.at[0, 1]), (k_ref, k_in.at[0, 0, 0]),
        (dk_ref, k_in.at[0, 0, 1]), (v_ref, k_in.at[0, 0, 2]), (dv_ref, k_in.at[0, 0, 3]),
    ):
        pltpu.make_async_copy(src.at[0], dst, own_sem).start()
    barrier = pltpu.get_barrier_semaphore()
    peers = (x_up, x_down, z_up, z_down, q_pair, k_pair, twin)
    for peer in peers:
        pl.semaphore_signal(barrier, inc=1, device_id=peer, device_id_type=MESH)

    lots = {}

    def message(lot, group, src, dst, peer):
        n = lots.setdefault(lot, len(lots))
        return pltpu.make_async_remote_copy(
            src_ref=src, dst_ref=dst, send_sem=send_sem.at[group], recv_sem=recv_sem.at[n],
            device_id=peer, device_id_type=MESH,
        )

    def arrive(lot, size):
        pltpu.make_async_remote_copy(
            src_ref=size, dst_ref=size, send_sem=send_sem.at[0], recv_sem=recv_sem.at[lots[lot]],
            device_id=twin, device_id_type=MESH,
        ).wait_recv()

    def arrays(lot, count, rows=B):
        arrive(lot, k_in.at[:count, 0, 0, :rows])

    def begin(*copies):
        for copy in copies:
            copy.start()

    def q_message(a, src, dst, peer, lot=None):
        return message(lot or ("q", dst, a), 0, q_in.at[src, a], q_in.at[dst, a], peer)

    q1, q2, q3 = ((0, 0, 1, x_up), (0, 0, 2, x_down), (0, 0, 3, q_pair))
    qm = {
        (1, 0): q_message(*q1), (1, 1): q_message(1, 0, 1, x_up),
        (2, 0): q_message(*q2, "q near"), (2, 1): q_message(1, 0, 2, x_down),
        (3, 0): q_message(*q3), (3, 1): q_message(1, 0, 3, q_pair, "q near"),
        (4, 0): q_message(0, 3, 4, x_up, "q far"), (5, 0): q_message(0, 3, 5, x_down),
        (6, 0): q_message(0, 1, 6, x_up, "q far"), (7, 0): q_message(0, 5, 7, x_down, "q far"),
        (4, 1): q_message(1, 1, 4, q_pair, "q far"), (5, 1): q_message(1, 2, 5, q_pair, "q far"),
        (6, 1): q_message(1, 1, 6, x_up), (7, 1): q_message(1, 6, 7, q_pair, "q far"),
    }

    def half(s, c, a, h):
        return k_in.at[s, c, a, pl.ds(h * H, H)]

    near_lots = {
        (1, 2): "v1", (1, 3): "dv1", (2, 2): "v2", (2, 3): "v2",
        (1, 0): "k12", (1, 1): "k12", (2, 0): "k12", (2, 1): "k12",
    }
    near = {
        (s, a, h): message(near_lots[s, a] if h else "k near", 1, half(0, 0, a, h), half(s, 0, a, h), peer)
        for s, peer in ((1, z_up), (2, z_down))
        for a in range(4)
        for h in range(2)
    }

    def k_message(a, src, dst, peer, lot):
        return message(lot, 1, k_in.at[src, 0, a], k_in.at[dst, 0, a], peer)

    km = {}
    for a in range(2):
        km[3, a] = k_message(a, 0, 3, k_pair, ("k3", a))
        km[3, 2 + a] = k_message(2 + a, 0, 3, k_pair, "v3")
        km[4, a] = k_message(a, 3, 4, z_up, "k45")
        km[5, a] = k_message(a, 3, 5, z_down, ("k5", a))
        km[6, a] = k_message(a, 1, 6, z_up, "k67")
        km[7, a] = k_message(a, 5, 7, z_down, "k67")
        v = 2 + a
        km[4, v] = k_message(v, 1, 4, k_pair, "k45")
        km[5, v] = k_message(v, 2, 5, k_pair, "k45")
        km[6, v] = k_message(v, 1 + a, 6, (z_up, z_down)[a], ("v6", a))
        km[7, v] = k_message(v, 6, 7, k_pair, "v7")
    tm = {0: message("t0", 2, k_in.at[0, 0], k_in.at[0, 1], twin)}
    for s in (1, 2):
        for h in range(2):
            rows = pl.ds(h * H, H)
            tm[s, h] = message(("t near", h), 2, k_in.at[s, 0, :, rows], k_in.at[s, 1, :, rows], twin)
    for s in (3, 4, 5, 6, 7):
        for h in range(2):
            pair = pl.ds(2 * h, 2)
            lot = {3: ("t near", 1), 4: "t4", 5: "t56", 6: "t56", 7: "t7"}[s]
            tm[s, h] = message(lot, 2, k_in.at[s, 0, pair], k_in.at[s, 1, pair], twin)

    def whole(lot, group, src, dst, peer):
        return [message(lot, group, src, dst, peer)]

    def halves(lot, group, src, dst, peer):
        return [
            message((lot, at), group, src.at[pl.ds(at, size)], dst.at[pl.ds(at, size)], peer)
            for at, size in HALVES
        ]

    nm = {
        "2": whole("n2", 3, num.at[6], num_in.at[0], x_up),
        "4": halves("n4", 3, num.at[7], num_in.at[1], x_down),
        "3a": whole("n3", 3, num.at[5], num_in.at[2], x_up),
        "3b": halves("n3b", 3, num.at[4], num_in.at[3], x_down),
        "0a": whole("n0", 3, num.at[2], num_in.at[4], x_up),
        "0b": whole("n0", 3, num.at[1], num_in.at[5], x_down),
        "0c": halves("n0c", 3, num.at[3], num_in.at[6], q_pair),
    }
    dm = {
        "6": halves("d6", 4, tan.at[7], tan_in.at[0], q_pair),
        "1": whole("d1", 4, tan.at[4], tan_in.at[1], q_pair),
        "2": whole("d2", 4, tan.at[5], tan_in.at[2], q_pair),
        "0": whole("d0", 4, tan.at[3], tan_in.at[3], q_pair),
        "2a": halves("d2a", 4, tan.at[6], tan_in.at[4], x_up),
        "0a": halves("d0a", 4, tan.at[2], tan_in.at[5], x_up),
        "0b": whole("d0", 4, tan.at[1], tan_in.at[6], x_down),
    }
    assert len(lots) == LOTS, len(lots)

    num[...] = jnp.zeros_like(num)
    tan[...] = jnp.zeros_like(tan)
    for s in range(8):
        num[s, STATS : STATS + 1] = jnp.full((1, B), -1e30, F32)
    own = k_in.at[:6, 0, 0]
    pltpu.make_async_copy(own, own, own_sem).wait()
    pl.semaphore_wait(barrier, len(peers))

    begin(qm[1, 1], qm[2, 1], qm[3, 0])
    for a in range(4):
        begin(km[3, a], near[1, a, 0], near[2, a, 0])
        if a == 0:
            begin(qm[1, 0], qm[2, 0], qm[3, 1], tm[0])
    for a in (2, 3, 0, 1):
        begin(near[1, a, 1], near[2, a, 1])

    scale = B**-0.5 * LOG2E

    def take_q(s):
        for a in range(2):
            high, low = split((q_in[s, a] * scale).T)
            qt[s, 2 * B * a : 2 * B * a + B] = high
            qt[s, 2 * B * a + B : 2 * B * a + 2 * B] = low

    def take_k(at, *parts):
        r = pl.ds(at * B, B)

        def read(a):
            got = [k_in[p[0], p[1], a] if len(p) == 2 else half(*p[:2], a, p[2])[...] for p in parts]
            return got[0] if len(got) == 1 else jnp.concatenate(got, axis=0)

        for a in range(2):
            high, low = split(read(a))
            kb[r, 2 * B * a : 2 * B * a + B] = high
            kb[r, 2 * B * a + B : 2 * B * a + 2 * B] = low
        for a in range(2):
            value = read(2 + a).T
            high, low = split(value * LOG2E if a else value)
            vt[2 * B * a : 2 * B * a + B, r] = high
            vt[2 * B * a + B : 2 * B * a + 2 * B, r] = low

    def step(first, blocks, side):
        r = pl.ds(pl.multiple_of(first * B, B), blocks * B)
        kk, dd = kb[r, : 2 * B], kb[r, 2 * B :]
        khigh = kk[:, :B]
        kd = jnp.concatenate([khigh, dd[:, :B]], axis=1)
        at = [side * 4 + j for j in range(4)]

        def wide(read):
            return jnp.concatenate([read(n) for n in at], axis=1)

        def sums(ref):
            return wide(lambda n: jnp.concatenate([ref[n, :H], ref[n, ROWS - H :]], axis=0))

        def stat(ref, row):
            return wide(lambda n: ref[n, STATS + row : STATS + row + 1])

        def put_sums(ref, value):
            for j, n in enumerate(at):
                ref[n, :H] = value[:H, j * B : (j + 1) * B]
                ref[n, ROWS - H :] = value[H:, j * B : (j + 1) * B]

        def put_stat(ref, row, value):
            for j, n in enumerate(at):
                ref[n, STATS + row : STATS + row + 1] = value[:, j * B : (j + 1) * B]

        qhigh, qlow, dqhigh, dqlow = (
            wide(lambda n: qt[n, m * B : (m + 1) * B]) for m in range(4)
        )
        qq = jnp.concatenate([qhigh, qhigh], axis=0)
        s_ = dot(kk, qq) + dot(khigh, qlow)
        t_ = (
            dot(kk, jnp.concatenate([dqhigh, dqhigh], axis=0))
            + dot(dd, qq)
            + dot(kd, jnp.concatenate([dqlow, qlow], axis=0))
        )
        old = stat(num, 0)
        new = jnp.maximum(old, jnp.max(s_, axis=0, keepdims=True))
        shrink = jnp.exp2(old - new)
        w = jnp.exp2(s_ - new)
        p = w * t_
        put_stat(num, 1, stat(num, 1) * shrink + jnp.sum(w, axis=0, keepdims=True))
        put_stat(tan, 1, stat(tan, 1) * shrink + jnp.sum(p, axis=0, keepdims=True))
        put_stat(num, 0, new)
        put_stat(tan, 0, new)
        whigh, wlow = split(w)
        phigh, plow = split(p)
        vhigh, vlow, dvhigh, dvlow = (vt[n * B : (n + 1) * B, r] for n in range(4))
        n_ = dot(vhigh, whigh) + dot(vlow, whigh) + dot(vhigh, wlow)
        d_ = (
            dot(dvhigh, whigh) + dot(dvlow, whigh) + dot(dvhigh, wlow)
            + dot(vhigh, phigh) + dot(vlow, phigh) + dot(vhigh, plow)
        )
        put_sums(num, sums(num) * shrink + n_)
        put_sums(tan, sums(tan) * shrink + d_)

    def early_0():
        take_q(0)
        take_k(0, (0, 0))
        arrays("t0", 4)
        take_k(1, (0, 1))
        arrays(("q", 1, 1), 1)
        begin(qm[6, 1], qm[4, 1])
        arrays(("q", 2, 1), 1)
        begin(qm[5, 1])
        arrays(("q", 3, 0), 1)
        begin(qm[4, 0], qm[5, 0])
        arrays(("q", 1, 0), 1)
        begin(qm[6, 0])
        arrays("q near", 2)
        arrays(("k3", 0), 1)
        begin(km[4, 0], km[5, 0])
        for s in (1, 2, 3):
            take_q(s)

    def early_1():
        arrays("k near", 4)
        begin(tm[1, 0], tm[2, 0])
        arrays(("k3", 1), 1)
        arrays("v1", 1, H)
        begin(km[6, 2], km[4, 2], km[4, 1], km[5, 1], tm[3, 0])
        take_k(2, (1, 0, 0), (2, 0, 0))
        arrays("dv1", 1, H)
        begin(km[4, 3])
        arrays("v2", 2, H)
        begin(km[6, 3], km[5, 2], km[5, 3])
        arrays(("q", 5, 0), 1)
        begin(qm[7, 0])
        arrays(("q", 6, 1), 1)
        begin(qm[7, 1])
        arrays(("t near", 0), 4)
        take_k(3, (1, 1, 0), (2, 1, 0))

    def early_2():
        arrays("k12", 4, H)
        begin(km[6, 0], km[6, 1], tm[1, 1], tm[2, 1])
        take_k(4, (1, 0, 1), (2, 0, 1))
        arrays("v3", 2)
        begin(tm[3, 1])
        take_k(5, (3, 0))

    def early_3():
        arrays(("t near", 1), 8)
        take_k(6, (1, 1, 1), (2, 1, 1))
        take_k(7, (3, 1))
        arrays(("k5", 0), 1)
        begin(km[7, 0])

    def late_0():
        arrays(("v6", 0), 1)
        begin(km[7, 2])
        arrays(("k5", 1), 1)
        begin(km[7, 1], tm[5, 0])
        arrays("q far", 6)
        for s in (4, 5, 6, 7):
            take_q(s)
        arrays(("v6", 1), 1)
        begin(km[7, 3], tm[6, 1])

    def late_1():
        arrays("k45", 6)
        begin(tm[4, 0], tm[4, 1], tm[5, 1])

    def late_2():
        arrays("k67", 4)
        begin(tm[6, 0], tm[7, 0])
        arrays("t4", 4)
        for n, block in enumerate(((4, 0), (4, 1), (5, 0), (6, 0))):
            take_k(8 + n, block)

    def last_0():
        arrays("v7", 2)
        begin(tm[7, 1])
        arrays("t56", 8)
        take_k(12, (5, 1))
        take_k(13, (6, 1))

    def last_1():
        arrays("t7", 4)
        take_k(14, (7, 0))
        take_k(15, (7, 1))

    def steps(events, first, blocks, side):
        def one(i, carry):
            for n, event in enumerate(events):
                pl.when(i == n)(event)
            step(first + blocks * i, blocks, side)
            return carry

        return one

    lax.fori_loop(0, 4, steps((early_0, early_1, early_2, early_3), 0, 2, 0), 0)
    lax.fori_loop(0, 3, steps((late_0, late_1, late_2), 0, 4, 1), 0)
    lax.fori_loop(0, 2, steps((last_0, last_1), 12, 2, 1), 0)
    begin(*nm["4"], *dm["6"], *nm["2"], *dm["1"], *nm["3a"], *dm["2"])
    lax.fori_loop(0, 2, steps((), 8, 4, 0), 0)

    def add(copies, ref, s, other, then=(), wait=None):
        if wait is not None:
            arrive(*wait)
        factors = None
        for n, (at, size) in enumerate(HALVES):
            if wait is None and n < len(copies):
                copies[n].wait_recv()
            r = pl.ds(at, size)
            if factors is None:
                old, got = ref[s, STATS : STATS + 1], other[STATS : STATS + 1]
                peak = jnp.maximum(old, got)
                factors = jnp.exp2(old - peak), jnp.exp2(got - peak)
            ref[s, r] = ref[s, r] * factors[0] + other[r] * factors[1]
            if n == 0:
                ref[s, STATS : STATS + 1] = peak
            if n >= len(HALVES) - len(then):
                begin(then[n - len(HALVES) + len(then)])

    begin(*dm["0"], *nm["0b"])
    add(dm["6"], tan, 6, tan_in.at[0], dm["2a"])
    add(nm["4"], num, 4, num_in.at[1], nm["3b"])
    add(nm["2"], num, 2, num_in.at[0], nm["0a"])
    add(dm["1"], tan, 1, tan_in.at[1], dm["0b"])
    add(dm["2"], tan, 2, tan_in.at[2])
    add(nm["3a"], num, 3, num_in.at[2])
    add(nm["3b"], num, 3, num_in.at[3], nm["0c"])
    add(dm["2a"], tan, 2, tan_in.at[4], dm["0a"])
    add(nm["0b"], num, 0, num_in.at[5], (), ("n0", num_in.at[:2]))
    add((), num, 0, num_in.at[4])
    add(dm["0"], tan, 0, tan_in.at[3], (), ("d0", tan_in.at[:2]))
    add((), tan, 0, tan_in.at[6])
    add(nm["0c"], num, 0, num_in.at[6])
    add(dm["0a"], tan, 0, tan_in.at[5])
    num_out[...] = num[0]
    tan_out[...] = tan[0]
    for group, size in enumerate((q_in.at[:7], k_in.at[:7, 0], k_in.at[:, 1], num_in, tan_in)):
        pltpu.make_async_remote_copy(
            src_ref=size, dst_ref=size, send_sem=send_sem.at[group], recv_sem=recv_sem.at[0],
            device_id=twin, device_id_type=MESH,
        ).wait_send()


def finish(num, tan, out_ref, tout_ref):
    inverse = 1.0 / num[STATS + 1 : STATS + 2]
    mean = tan[STATS + 1 : STATS + 2] * inverse
    for h, at in enumerate((0, ROWS - H)):
        attended = num[at : at + H] * inverse
        moved = (tan[at : at + H] * inverse - attended * mean) * (1.0 / LOG2E)
        out_ref[0, :, h * H : (h + 1) * H] = attended.T
        tout_ref[0, :, h * H : (h + 1) * H] = moved.T


def body(*args):
    sums = jax.ShapeDtypeStruct((ROWS, B), F32)
    shape = jax.ShapeDtypeStruct((1, B, B), F32)
    vmem = pl.BlockSpec(memory_space=pltpu.VMEM)
    sums = pl.pallas_call(
        kernel,
        out_shape=[sums, sums],
        in_specs=[pl.BlockSpec(memory_space=pltpu.HBM)] * 6,
        out_specs=[vmem, vmem],
        scratch_shapes=[
            pltpu.VMEM((8, 2, B, B), F32),
            pltpu.VMEM((8, 2, 4, B, B), F32),
            pltpu.VMEM((8, 4 * B, B), BF16),
            pltpu.VMEM((16 * B, 4 * B), BF16),
            pltpu.VMEM((4 * B, 16 * B), BF16),
            pltpu.VMEM((8, ROWS, B), F32),
            pltpu.VMEM((8, ROWS, B), F32),
            pltpu.VMEM((7, ROWS, B), F32),
            pltpu.VMEM((7, ROWS, B), F32),
            pltpu.SemaphoreType.DMA,
            pltpu.SemaphoreType.DMA((5,)),
            pltpu.SemaphoreType.DMA((LOTS,)),
        ],
        compiler_params=pltpu.CompilerParams(
            collective_id=0, has_side_effects=True, vmem_limit_bytes=32 << 20
        ),
    )(*(pltpu.with_memory_space_constraint(a, pltpu.HBM) for a in args))
    return pl.pallas_call(
        finish,
        out_shape=[shape, shape],
        in_specs=[vmem, vmem],
        out_specs=[vmem, vmem],
        compiler_params=pltpu.CompilerParams(vmem_limit_bytes=4 << 20),
    )(*sums)


def solution(mesh):
    rows, columns = P(None, ("pb", "ka"), None), P(None, ("ka", "pb"), None)
    return jax.shard_map(
        body,
        mesh=mesh,
        in_specs=(rows, columns, columns, rows, columns, columns),
        out_specs=(rows, rows),
        check_vma=False,
    )
```

time: 227 us -> 41.1 us (0.18)
  waiting for transfers between devices: 71.7 us -> 0 us
  matrix products: 70.1 us -> 0 us
  blocking collectives: 46.1 us -> 0 us
  Pallas kernels: 0 us -> 40.3 us
  local copies, waits for them, and re-layouts: 15.5 us -> 0 us
  between operations: 14.2 us -> 0.64 us
  other arithmetic: 8.42 us -> 0 us
    all_gather x2 -> x0, waiting for transfers between devices: 71.7 us -> none  [sent_together(): lax.all_gather(both, axis, axis=dim, tiled=True)]
    dot_general x24 -> x0, matrix products: 70.1 us -> none  [the longest x4 18.4 us: one_block(): jnp.dot(query_blk, head_dk.T, precision=highest)]
    pallas_call x0 -> x2, Pallas kernels: none -> 40.3 us  [the longest x1 39.4 us: body(): pl.pallas_call(kernel, out_shape=[sums, sums], in_specs=[pl.BlockSpec(mem...]
    all_to_all x1 -> x0, blocking collectives: 27.1 us -> none  [sum_at_owner(): blocks = lax.all_to_all(split_up(x, dim, peers), axis, 0, 0, tiled=True)]
    pmax x2 -> x0, blocking collectives: 19 us -> none  [by_axis(): return functools.reduce(lax.pmax, axes, x)]
    concatenate x3 -> x0, local copies, waits for them, and re-layouts: 6.58 us -> none  [sent_together_2(): jnp.concatenate([a.reshape(*a.shape[:along], w) for a, w in zip(arrays, w...]
    concatenate x3 -> x0, other arithmetic: 4.59 us -> none  [the longest x2 3.18 us: sent_together(): both = jnp.concatenate(arrays, axis=along)]
    reduce_sum x5 -> x0, other arithmetic: 3.3 us -> none  [the longest x4 2 us: one_block(): new_total = old_total * rescale + jnp.sum(weights, axis=1)]
  transfers between devices with their start and end apart: 2 -> 0, of which waited for: 2 -> 0; matrix products, arithmetic and copies ran while one was open for 2% -> 0% of each run, Pallas kernels for 0% -> 0%
where the time goes in v1:
time: 41.1 us; the launch traced here: 40.9 us
  Pallas kernels  40.3 us (98%)
  between operations  0.64 us (2%)
    pallas_call x1, Pallas kernels, body(): pl.pallas_call(kernel, out_shape=[sums, sums], in_specs=[pl.BlockSpec(mem...  39.4 us
    pallas_call x1, Pallas kernels, body(): pl.pallas_call(finish, out_shape=[shape, shape], in_specs=[vmem, vmem], o...  0.91 us

profile of v1, /device:TPU:0, one launch (start us, length us, event | category | flops | bytes accessed | tf_op | source)
XLA Modules:
  0.0 40.9 jit_solution(16588851062093096263)
XLA Ops:
  0.6 39.4 %shard_map.77 = (f32[136,128]{1,0:T(8,128)S(1)}, f32[136,128]{1,0:T(8,128)S(1)}) custom-call(f32[1,128,128]{2,1,0:T(8,128)} %q_ref.1, f32[1,128,128]{2,1,0:T(8,128)} %k_ref.1, f32[1,128,128]{2,1,0:T(8,128)} %v_ref.1, f32[1,128,128]{2,1,0:T(8,128)} %dq_ref.1, f32[1,128,128]{2,1,0:T(8,128)} %dk_ref.1, f32[1,128,128]{2,1,0:T(8,128)} %dv_ref.1), custom_call_target="tpu_custom_call" | custom-call | tf_op jit(solution)/shard_map/pallas_call | solution.py:413
  40.0 0.9 %shard_map.78 = (f32[1,128,128]{2,1,0:T(8,128)}, f32[1,128,128]{2,1,0:T(8,128)}) custom-call(f32[136,128]{1,0:T(8,128)S(1)} %get-tuple-element.4.num, f32[136,128]{1,0:T(8,128)S(1)} %get-tuple-element.5.tan), custom_call_target="tpu_custom_call" | custom-call | tf_op jit(solution)/shard_map/pallas_call | solution.py:436

commit v2 on v1

--- a/solution.py
+++ b/solution.py
@@ -354,39 +354,47 @@
     begin(*nm["4"], *dm["6"], *nm["2"], *dm["1"], *nm["3a"], *dm["2"])
     lax.fori_loop(0, 2, steps((), 8, 4, 0), 0)
 
-    def add(copies, ref, s, other, then=(), wait=None):
-        if wait is not None:
-            arrive(*wait)
-        factors = None
+    def join(ref, s, other):
+        old, got = ref[s, STATS : STATS + 1], other[STATS : STATS + 1]
+        peak = jnp.maximum(old, got)
+        mine, theirs = jnp.exp2(old - peak), jnp.exp2(got - peak)
         for n, (at, size) in enumerate(HALVES):
-            if wait is None and n < len(copies):
-                copies[n].wait_recv()
             r = pl.ds(at, size)
-            if factors is None:
-                old, got = ref[s, STATS : STATS + 1], other[STATS : STATS + 1]
-                peak = jnp.maximum(old, got)
-                factors = jnp.exp2(old - peak), jnp.exp2(got - peak)
-            ref[s, r] = ref[s, r] * factors[0] + other[r] * factors[1]
+            ref[s, r] = ref[s, r] * mine + other[r] * theirs
             if n == 0:
                 ref[s, STATS : STATS + 1] = peak
-            if n >= len(HALVES) - len(then):
-                begin(then[n - len(HALVES) + len(then)])
-
-    begin(*dm["0"], *nm["0b"])
-    add(dm["6"], tan, 6, tan_in.at[0], dm["2a"])
-    add(nm["4"], num, 4, num_in.at[1], nm["3b"])
+                yield
+
+    def add(copies, ref, s, other, then=()):
+        for copy in copies:
+            copy.wait_recv()
+        for _ in join(ref, s, other):
+            pass
+        begin(*then)
+
+    def relay(*chains):
+        joins = [join(ref, s, other) for _, ref, s, other, _ in chains]
+        for n in range(2):
+            for part, (copies, _, _, _, then) in zip(joins, chains):
+                copies[n].wait_recv()
+                next(part, None)
+                begin(*then[n : n + 1])
+
+    begin(*dm["0"])
+    relay((dm["6"], tan, 6, tan_in.at[0], dm["2a"]), (nm["4"], num, 4, num_in.at[1], nm["3b"]))
+    begin(*nm["0b"])
     add(nm["2"], num, 2, num_in.at[0], nm["0a"])
     add(dm["1"], tan, 1, tan_in.at[1], dm["0b"])
+    add(nm["3a"], num, 3, num_in.at[2])
     add(dm["2"], tan, 2, tan_in.at[2])
-    add(nm["3a"], num, 3, num_in.at[2])
-    add(nm["3b"], num, 3, num_in.at[3], nm["0c"])
-    add(dm["2a"], tan, 2, tan_in.at[4], dm["0a"])
-    add(nm["0b"], num, 0, num_in.at[5], (), ("n0", num_in.at[:2]))
+    relay((dm["2a"], tan, 2, tan_in.at[4], dm["0a"]), (nm["3b"], num, 3, num_in.at[3], nm["0c"]))
+    arrive("n0", num_in.at[:2])
+    add((), num, 0, num_in.at[5])
     add((), num, 0, num_in.at[4])
-    add(dm["0"], tan, 0, tan_in.at[3], (), ("d0", tan_in.at[:2]))
+    relay((dm["0a"], tan, 0, tan_in.at[5], ()), (nm["0c"], num, 0, num_in.at[6], ()))
+    arrive("d0", tan_in.at[:2])
+    add((), tan, 0, tan_in.at[3])
     add((), tan, 0, tan_in.at[6])
-    add(nm["0c"], num, 0, num_in.at[6])
-    add(dm["0a"], tan, 0, tan_in.at[5])
     num_out[...] = num[0]
     tan_out[...] = tan[0]
     for group, size in enumerate((q_in.at[:7], k_in.at[:7, 0], k_in.at[:, 1], num_in, tan_in)):

time: 41.1 us -> 39.5 us (0.961); the launches traced: 40.9 us -> 38.9 us
  Pallas kernels: 40.3 us -> 38.2 us
    pallas_call x1, Pallas kernels: 39.4 us -> 37.3 us  [body(): pl.pallas_call(kernel, out_shape=[sums, sums], in_specs=[pl.BlockSpec(mem...]
where the time goes in v2:
time: 39.5 us; the launch traced here: 38.9 us
  Pallas kernels  38.2 us (97%)
  between operations  0.64 us (2%)
    pallas_call x1, Pallas kernels, body(): pl.pallas_call(kernel, out_shape=[sums, sums], in_specs=[pl.BlockSpec(mem...  37.3 us
    pallas_call x1, Pallas kernels, body(): pl.pallas_call(finish, out_shape=[shape, shape], in_specs=[vmem, vmem], o...  0.91 us

profile of v2, /device:TPU:0, one launch (start us, length us, event | category | flops | bytes accessed | tf_op | source)
XLA Modules:
  0.0 38.9 jit_solution(14951550918536476896)
XLA Ops:
  0.6 37.3 %shard_map.77 = (f32[136,128]{1,0:T(8,128)S(1)}, f32[136,128]{1,0:T(8,128)S(1)}) custom-call(f32[1,128,128]{2,1,0:T(8,128)} %q_ref.1, f32[1,128,128]{2,1,0:T(8,128)} %k_ref.1, f32[1,128,128]{2,1,0:T(8,128)} %v_ref.1, f32[1,128,128]{2,1,0:T(8,128)} %dq_ref.1, f32[1,128,128]{2,1,0:T(8,128)} %dk_ref.1, f32[1,128,128]{2,1,0:T(8,128)} %dv_ref.1), custom_call_target="tpu_custom_call" | custom-call | tf_op jit(solution)/shard_map/pallas_call | solution.py:421
  38.0 0.9 %shard_map.78 = (f32[1,128,128]{2,1,0:T(8,128)}, f32[1,128,128]{2,1,0:T(8,128)}) custom-call(f32[136,128]{1,0:T(8,128)S(1)} %get-tuple-element.4.num, f32[136,128]{1,0:T(8,128)S(1)} %get-tuple-element.5.tan), custom_call_target="tpu_custom_call" | custom-call | tf_op jit(solution)/shard_map/pallas_call | solution.py:444

commit v3 on v2

--- a/solution.py
+++ b/solution.py
@@ -11,10 +11,10 @@
 MESH = pl.DeviceIdType.MESH
 B = 128
 H = 64
-ROWS, STATS = 136, 64
-HALVES = ((0, 72), (72, 64))
+ROWS, DATA = 136, 8
+PIECES = ((0, 72), (72, 64))
 LOG2E = math.log2(math.e)
-LOTS = 47
+LOTS = 50
 
 
 def split(x):
@@ -82,9 +82,9 @@
         (2, 0): q_message(*q2, "q near"), (2, 1): q_message(1, 0, 2, x_down),
         (3, 0): q_message(*q3), (3, 1): q_message(1, 0, 3, q_pair, "q near"),
         (4, 0): q_message(0, 3, 4, x_up, "q far"), (5, 0): q_message(0, 3, 5, x_down),
-        (6, 0): q_message(0, 1, 6, x_up, "q far"), (7, 0): q_message(0, 5, 7, x_down, "q far"),
+        (6, 0): q_message(0, 1, 6, x_up, "q far"), (7, 0): q_message(0, 5, 7, x_down, "q 7"),
         (4, 1): q_message(1, 1, 4, q_pair, "q far"), (5, 1): q_message(1, 2, 5, q_pair, "q far"),
-        (6, 1): q_message(1, 1, 6, x_up), (7, 1): q_message(1, 6, 7, q_pair, "q far"),
+        (6, 1): q_message(1, 1, 6, x_up), (7, 1): q_message(1, 6, 7, q_pair, "q 7"),
     }
 
     def half(s, c, a, h):
@@ -108,13 +108,13 @@
     for a in range(2):
         km[3, a] = k_message(a, 0, 3, k_pair, ("k3", a))
         km[3, 2 + a] = k_message(2 + a, 0, 3, k_pair, "v3")
-        km[4, a] = k_message(a, 3, 4, z_up, "k45")
+        km[4, a] = k_message(a, 3, 4, z_up, "k4")
         km[5, a] = k_message(a, 3, 5, z_down, ("k5", a))
-        km[6, a] = k_message(a, 1, 6, z_up, "k67")
-        km[7, a] = k_message(a, 5, 7, z_down, "k67")
+        km[6, a] = k_message(a, 1, 6, z_up, "k6")
+        km[7, a] = k_message(a, 5, 7, z_down, "k7")
         v = 2 + a
-        km[4, v] = k_message(v, 1, 4, k_pair, "k45")
-        km[5, v] = k_message(v, 2, 5, k_pair, "k45")
+        km[4, v] = k_message(v, 1, 4, k_pair, "k4")
+        km[5, v] = k_message(v, 2, 5, k_pair, "v5")
         km[6, v] = k_message(v, 1 + a, 6, (z_up, z_down)[a], ("v6", a))
         km[7, v] = k_message(v, 6, 7, k_pair, "v7")
     tm = {0: message("t0", 2, k_in.at[0, 0], k_in.at[0, 1], twin)}
@@ -131,28 +131,28 @@
     def whole(lot, group, src, dst, peer):
         return [message(lot, group, src, dst, peer)]
 
-    def halves(lot, group, src, dst, peer):
+    def pieces(lot, group, src, dst, peer):
         return [
             message((lot, at), group, src.at[pl.ds(at, size)], dst.at[pl.ds(at, size)], peer)
-            for at, size in HALVES
+            for at, size in PIECES
         ]
 
     nm = {
         "2": whole("n2", 3, num.at[6], num_in.at[0], x_up),
-        "4": halves("n4", 3, num.at[7], num_in.at[1], x_down),
+        "4": pieces("n4", 3, num.at[7], num_in.at[1], x_down),
         "3a": whole("n3", 3, num.at[5], num_in.at[2], x_up),
-        "3b": halves("n3b", 3, num.at[4], num_in.at[3], x_down),
+        "3b": pieces("n3b", 3, num.at[4], num_in.at[3], x_down),
         "0a": whole("n0", 3, num.at[2], num_in.at[4], x_up),
         "0b": whole("n0", 3, num.at[1], num_in.at[5], x_down),
-        "0c": halves("n0c", 3, num.at[3], num_in.at[6], q_pair),
+        "0c": pieces("n0c", 3, num.at[3], num_in.at[6], q_pair),
     }
     dm = {
-        "6": halves("d6", 4, tan.at[7], tan_in.at[0], q_pair),
+        "6": pieces("d6", 4, tan.at[7], tan_in.at[0], q_pair),
         "1": whole("d1", 4, tan.at[4], tan_in.at[1], q_pair),
         "2": whole("d2", 4, tan.at[5], tan_in.at[2], q_pair),
         "0": whole("d0", 4, tan.at[3], tan_in.at[3], q_pair),
-        "2a": halves("d2a", 4, tan.at[6], tan_in.at[4], x_up),
-        "0a": halves("d0a", 4, tan.at[2], tan_in.at[5], x_up),
+        "2a": pieces("d2a", 4, tan.at[6], tan_in.at[4], x_up),
+        "0a": pieces("d0a", 4, tan.at[2], tan_in.at[5], x_up),
         "0b": whole("d0", 4, tan.at[1], tan_in.at[6], x_down),
     }
     assert len(lots) == LOTS, len(lots)
@@ -160,7 +160,7 @@
     num[...] = jnp.zeros_like(num)
     tan[...] = jnp.zeros_like(tan)
     for s in range(8):
-        num[s, STATS : STATS + 1] = jnp.full((1, B), -1e30, F32)
+        num[s, :1] = jnp.full((1, B), -1e30, F32)
     own = k_in.at[:6, 0, 0]
     pltpu.make_async_copy(own, own, own_sem).wait()
     pl.semaphore_wait(barrier, len(peers))
@@ -209,19 +209,18 @@
             return jnp.concatenate([read(n) for n in at], axis=1)
 
         def sums(ref):
-            return wide(lambda n: jnp.concatenate([ref[n, :H], ref[n, ROWS - H :]], axis=0))
+            return wide(lambda n: ref[n, DATA:])
 
         def stat(ref, row):
-            return wide(lambda n: ref[n, STATS + row : STATS + row + 1])
+            return wide(lambda n: ref[n, row : row + 1])
 
         def put_sums(ref, value):
             for j, n in enumerate(at):
-                ref[n, :H] = value[:H, j * B : (j + 1) * B]
-                ref[n, ROWS - H :] = value[H:, j * B : (j + 1) * B]
+                ref[n, DATA:] = value[:, j * B : (j + 1) * B]
 
         def put_stat(ref, row, value):
             for j, n in enumerate(at):
-                ref[n, STATS + row : STATS + row + 1] = value[:, j * B : (j + 1) * B]
+                ref[n, row : row + 1] = value[:, j * B : (j + 1) * B]
 
         qhigh, qlow, dqhigh, dqlow = (
             wide(lambda n: qt[n, m * B : (m + 1) * B]) for m in range(4)
@@ -308,26 +307,32 @@
     def late_0():
         arrays(("v6", 0), 1)
         begin(km[7, 2])
+        arrays("q far", 4)
+        for s in (4, 5, 6):
+            take_q(s)
         arrays(("k5", 1), 1)
         begin(km[7, 1], tm[5, 0])
-        arrays("q far", 6)
-        for s in (4, 5, 6, 7):
-            take_q(s)
+        arrays("q 7", 2)
+        take_q(7)
         arrays(("v6", 1), 1)
         begin(km[7, 3], tm[6, 1])
 
     def late_1():
-        arrays("k45", 6)
-        begin(tm[4, 0], tm[4, 1], tm[5, 1])
+        arrays("k4", 4)
+        begin(tm[4, 0], tm[4, 1])
 
     def late_2():
-        arrays("k67", 4)
-        begin(tm[6, 0], tm[7, 0])
+        arrays("v5", 2)
+        begin(tm[5, 1])
+        arrays("k6", 2)
+        begin(tm[6, 0])
         arrays("t4", 4)
         for n, block in enumerate(((4, 0), (4, 1), (5, 0), (6, 0))):
             take_k(8 + n, block)
 
     def last_0():
+        arrays("k7", 2)
+        begin(tm[7, 0])
         arrays("v7", 2)
         begin(tm[7, 1])
         arrays("t56", 8)
@@ -355,15 +360,15 @@
     lax.fori_loop(0, 2, steps((), 8, 4, 0), 0)
 
     def join(ref, s, other):
-        old, got = ref[s, STATS : STATS + 1], other[STATS : STATS + 1]
+        old, got = ref[s, :1], other[:1]
         peak = jnp.maximum(old, got)
         mine, theirs = jnp.exp2(old - peak), jnp.exp2(got - peak)
-        for n, (at, size) in enumerate(HALVES):
+        for n, (at, size) in enumerate(PIECES):
             r = pl.ds(at, size)
             ref[s, r] = ref[s, r] * mine + other[r] * theirs
             if n == 0:
-                ref[s, STATS : STATS + 1] = peak
-                yield
+                ref[s, :1] = peak
+            yield
 
     def add(copies, ref, s, other, then=()):
         for copy in copies:
@@ -374,7 +379,7 @@
 
     def relay(*chains):
         joins = [join(ref, s, other) for _, ref, s, other, _ in chains]
-        for n in range(2):
+        for n in range(len(PIECES)):
             for part, (copies, _, _, _, then) in zip(joins, chains):
                 copies[n].wait_recv()
                 next(part, None)
@@ -405,13 +410,11 @@
 
 
 def finish(num, tan, out_ref, tout_ref):
-    inverse = 1.0 / num[STATS + 1 : STATS + 2]
-    mean = tan[STATS + 1 : STATS + 2] * inverse
-    for h, at in enumerate((0, ROWS - H)):
-        attended = num[at : at + H] * inverse
-        moved = (tan[at : at + H] * inverse - attended * mean) * (1.0 / LOG2E)
-        out_ref[0, :, h * H : (h + 1) * H] = attended.T
-        tout_ref[0, :, h * H : (h + 1) * H] = moved.T
+    inverse = 1.0 / num[1:2]
+    attended = num[DATA:] * inverse
+    moved = (tan[DATA:] * inverse - attended * (tan[1:2] * inverse)) * (1.0 / LOG2E)
+    out_ref[0] = attended.T
+    tout_ref[0] = moved.T
 
 
 def body(*args):

time: 39.5 us -> 39.2 us (level)
  no operation moved by 1% of the time
where the time goes in v3:
time: 39.2 us; the launch traced here: 38.8 us
  Pallas kernels  38.1 us (97%)
  between operations  0.64 us (2%)
    pallas_call x1, Pallas kernels, body(): pl.pallas_call(kernel, out_shape=[sums, sums], in_specs=[pl.BlockSpec(mem...  37.4 us

profile of v3, /device:TPU:0, one launch (start us, length us, event | category | flops | bytes accessed | tf_op | source)
XLA Modules:
  0.0 38.8 jit_solution(10341616126532862016)
XLA Ops:
  0.6 37.4 %shard_map.77 = (f32[136,128]{1,0:T(8,128)S(1)}, f32[136,128]{1,0:T(8,128)S(1)}) custom-call(f32[1,128,128]{2,1,0:T(8,128)} %q_ref.1, f32[1,128,128]{2,1,0:T(8,128)} %k_ref.1, f32[1,128,128]{2,1,0:T(8,128)} %v_ref.1, f32[1,128,128]{2,1,0:T(8,128)} %dq_ref.1, f32[1,128,128]{2,1,0:T(8,128)} %dk_ref.1, f32[1,128,128]{2,1,0:T(8,128)} %dv_ref.1), custom_call_target="tpu_custom_call" | custom-call | tf_op jit(solution)/shard_map/pallas_call | solution.py:424
  38.0 0.8 %shard_map.78 = (f32[1,128,128]{2,1,0:T(8,128)}, f32[1,128,128]{2,1,0:T(8,128)}) custom-call(f32[136,128]{1,0:T(8,128)S(1)} %get-tuple-element.4.num, f32[136,128]{1,0:T(8,128)S(1)} %get-tuple-element.5.tan), custom_call_target="tpu_custom_call" | custom-call | tf_op jit(solution)/shard_map/pallas_call | solution.py:447

commit v4 on v3

--- a/solution.py
+++ b/solution.py
@@ -388,8 +388,8 @@
     begin(*dm["0"])
     relay((dm["6"], tan, 6, tan_in.at[0], dm["2a"]), (nm["4"], num, 4, num_in.at[1], nm["3b"]))
     begin(*nm["0b"])
+    add(dm["1"], tan, 1, tan_in.at[1], dm["0b"])
     add(nm["2"], num, 2, num_in.at[0], nm["0a"])
-    add(dm["1"], tan, 1, tan_in.at[1], dm["0b"])
     add(nm["3a"], num, 3, num_in.at[2])
     add(dm["2"], tan, 2, tan_in.at[2])
     relay((dm["2a"], tan, 2, tan_in.at[4], dm["0a"]), (nm["3b"], num, 3, num_in.at[3], nm["0c"]))

time: 39.2 us -> 39.2 us (level)
  no operation moved by 1% of the time
where the time goes in v4:
time: 39.2 us; the launch traced here: 38.6 us
  Pallas kernels  38 us (97%)
  between operations  0.64 us (2%)
    pallas_call x1, Pallas kernels, body(): pl.pallas_call(kernel, out_shape=[sums, sums], in_specs=[pl.BlockSpec(mem...  37.2 us

profile of v4, /device:TPU:0, one launch (start us, length us, event | category | flops | bytes accessed | tf_op | source)
XLA Modules:
  0.0 38.6 jit_solution(16405555031920274924)
XLA Ops:
  0.6 37.2 %shard_map.77 = (f32[136,128]{1,0:T(8,128)S(1)}, f32[136,128]{1,0:T(8,128)S(1)}) custom-call(f32[1,128,128]{2,1,0:T(8,128)} %q_ref.1, f32[1,128,128]{2,1,0:T(8,128)} %k_ref.1, f32[1,128,128]{2,1,0:T(8,128)} %v_ref.1, f32[1,128,128]{2,1,0:T(8,128)} %dq_ref.1, f32[1,128,128]{2,1,0:T(8,128)} %dk_ref.1, f32[1,128,128]{2,1,0:T(8,128)} %dv_ref.1), custom_call_target="tpu_custom_call" | custom-call | tf_op jit(solution)/shard_map/pallas_call | solution.py:424
  37.8 0.8 %shard_map.78 = (f32[1,128,128]{2,1,0:T(8,128)}, f32[1,128,128]{2,1,0:T(8,128)}) custom-call(f32[136,128]{1,0:T(8,128)S(1)} %get-tuple-element.4.num, f32[136,128]{1,0:T(8,128)S(1)} %get-tuple-element.5.tan), custom_call_target="tpu_custom_call" | custom-call | tf_op jit(solution)/shard_map/pallas_call | solution.py:447

commit v5 on v3

--- a/solution.py
+++ b/solution.py
@@ -226,7 +226,7 @@
             wide(lambda n: qt[n, m * B : (m + 1) * B]) for m in range(4)
         )
         qq = jnp.concatenate([qhigh, qhigh], axis=0)
-        s_ = dot(kk, qq) + dot(khigh, qlow)
+        s_ = dot(kk, qq) + dot(kk, jnp.concatenate([qlow, qlow], axis=0))
         t_ = (
             dot(kk, jnp.concatenate([dqhigh, dqhigh], axis=0))
             + dot(dd, qq)

time: 39.2 us -> 39.3 us (level)
  no operation moved by 1% of the time
where the time goes in v5:
time: 39.3 us; the launch traced here: 38.8 us
  Pallas kernels  38.2 us (97%)
  between operations  0.64 us (2%)
    pallas_call x1, Pallas kernels, body(): pl.pallas_call(kernel, out_shape=[sums, sums], in_specs=[pl.BlockSpec(mem...  37.4 us

profile of v5, /device:TPU:0, one launch (start us, length us, event | category | flops | bytes accessed | tf_op | source)
XLA Modules:
  0.0 38.8 jit_solution(3348198434394961715)
XLA Ops:
  0.6 37.4 %shard_map.77 = (f32[136,128]{1,0:T(8,128)S(1)}, f32[136,128]{1,0:T(8,128)S(1)}) custom-call(f32[1,128,128]{2,1,0:T(8,128)} %q_ref.1, f32[1,128,128]{2,1,0:T(8,128)} %k_ref.1, f32[1,128,128]{2,1,0:T(8,128)} %v_ref.1, f32[1,128,128]{2,1,0:T(8,128)} %dq_ref.1, f32[1,128,128]{2,1,0:T(8,128)} %dk_ref.1, f32[1,128,128]{2,1,0:T(8,128)} %dv_ref.1), custom_call_target="tpu_custom_call" | custom-call | tf_op jit(solution)/shard_map/pallas_call | solution.py:424
  38.0 0.8 %shard_map.78 = (f32[1,128,128]{2,1,0:T(8,128)}, f32[1,128,128]{2,1,0:T(8,128)}) custom-call(f32[136,128]{1,0:T(8,128)S(1)} %get-tuple-element.4.num, f32[136,128]{1,0:T(8,128)S(1)} %get-tuple-element.5.tan), custom_call_target="tpu_custom_call" | custom-call | tf_op jit(solution)/shard_map/pallas_call | solution.py:447
